TPU v7x, 256 devices: a whole 4x4x8 slice. The times are simulated.
256 devices in a mesh: gx: 8 (over z_hi, core), gy: 4 (over y), gz: 8 (over z_lo, x).
Axes of the slice: x: 4, y: 4, z: 8 (z_hi: 4, z_lo: 2; z = z_hi * 2 + z_lo), core: 2. Of those that a mesh axis runs over, the one named last changes fastest.
Arguments:
- field: float32 [256, 1024, 512], P('gz', 'gx', 'gy'), may hold values from -48 to 48
- factor_a: float32 [1024, 1024], replicated, may hold values from -0.5 to 3.5
- factor_b: float32 [512, 512], replicated, may hold values from -0.5 to 3.5
- factor_c: float32 [256, 256], replicated, may hold values from -0.5 to 3.5
Outputs:
- propagated: float32 [256, 1024, 512], P('gz', 'gx', 'gy')
All inputs are finite; a program needn't handle non-finite values.
Results may differ from a plain program's by a relative error of at most 0.00007.
Values sent between devices are 32-bit elements; how exact they have to be, the bound alone decides.
No kernel may reach another device: no remote copies, remote signals or barrier semaphores. Data moves between devices by JAX's collectives and lax.ppermute only.
A program may use at most 64 MiB of HBM per device.

v0:
```python
import jax
import jax.numpy as jnp
from jax import lax
from jax.sharding import Mesh
from jax.sharding import PartitionSpec as P

GX = ("gx_0", "gx_1")
GX_GY = ("gx_0", "gx_1", "gy")
GZ = ("gz_0", "gz_1")
GX_GY_GZ = ("gx_0", "gx_1", "gy", "gz_0", "gz_1")
epsilon = 1e-06
target_ratio = 0.5


def split_up(value, dim, size):
    dims = value.shape
    tiles = value.reshape(*dims[:dim], size, dims[dim] // size, *dims[dim + 1 :])
    return jnp.moveaxis(tiles, dim, 0)


def laid_out(tiles, dim):
    dims = list(tiles.shape[1:])
    dims[dim] *= tiles.shape[0]
    return jnp.moveaxis(tiles, 0, dim).reshape(dims)


def joined_exchange(value, axis, axes, splits, concats):
    sizes = [lax.axis_size(a) for a in axes]
    tiles = split_up(value, splits[0], sizes[0])
    tiles = jnp.moveaxis(split_up(tiles, splits[1] + 1, sizes[1]), 0, 1)
    inside = tiles.shape[2:]
    tiles = tiles.reshape(-1, *inside)
    tiles = lax.all_to_all(tiles, axis, split_axis=0, concat_axis=0, tiled=True)
    tiles = laid_out(tiles.reshape(*sizes, *inside), concats[0] + 1)
    return laid_out(tiles, concats[1])


def over_axes(value, axes):
    for axis in axes:
        value = lax.psum(value, axis)
    return value


def on_device(field, factor_a, factor_b, factor_c):
    highest = lax.Precision.HIGHEST
    count_x = lax.axis_size(GX)
    count_y = lax.axis_size("gy")

    def slab_products(slabs):
        along_one = jnp.einsum("ip,mpj->mij", factor_a, slabs, precision=highest)
        along_two = jnp.einsum("mip,jp->mij", slabs, factor_b, precision=highest)
        return along_one + along_two

    def plane_terms(tensor):
        depth_home, width_one, width_two = tensor.shape
        depth = depth_home // (count_x * count_y)
        slabs = joined_exchange(tensor, GX_GY, (GX, "gy"), (0, 0), (1, 2))
        products = slab_products(slabs)
        returned = joined_exchange(products, GX_GY, (GX, "gy"), (1, 2), (0, 0))
        returned = returned.reshape(count_y, count_x, depth, width_one, width_two)
        return returned.transpose(1, 0, 2, 3, 4).reshape(depth_home, width_one, width_two)

    def fibre_product(fibres):
        flat = fibres.reshape(fibres.shape[0], -1)
        product = jnp.dot(factor_c, flat, precision=highest).reshape(fibres.shape)
        return lax.all_to_all(product, GZ, split_axis=0, concat_axis=1, tiled=True)

    def apply_block(tensor):
        planes = plane_terms(tensor)
        fibres = fibre_product(lax.all_to_all(tensor, GZ, split_axis=1, concat_axis=0, tiled=True))
        return planes + fibres

    first_term = apply_block(field)
    size_field, size_first = (
        over_axes(jnp.sum(field * field), GX_GY_GZ),
        over_axes(jnp.sum(first_term * first_term), GX_GY_GZ),
    )
    step = target_ratio * jnp.sqrt(size_field / (size_first + epsilon))
    second_term = apply_block(first_term)
    result = field - step * first_term + step * step / 2.0 * second_term
    return result


def solution(mesh):
    finer = Mesh(
        mesh.devices.reshape(4, 2, mesh.shape["gy"], 2, 4), ("gx_0", "gx_1", "gy", "gz_0", "gz_1")
    )
    in_specs = (P(GZ, GX, "gy"), P(), P(), P())
    out_specs = P(GZ, GX, "gy")
    return jax.shard_map(
        on_device, mesh=finer, in_specs=in_specs, out_specs=out_specs, check_vma=False
    )
```

profile of v0, /device:TPU:32, one launch (start us, length us, event | category | flops | bytes accessed | tf_op | source)
XLA Modules:
  0.0 407.0 jit_solution(6824693490417956613)
XLA Ops:
  2.9 31.4 %all_to_all.89 = f32[32,128,128]{2,0,1:T(8,128)} all-to-all(f32[32,128,128]{2,0,1:T(8,128)S(1)} %copy.44), channel_id=1, replica_groups=mesh['gx_0'=4,'gx_1'=2,'gy'=4,'gz_0'=2,'gz_1'=4] {'gz_0','gz_1'}, dimensions={1} | all-to-all | bytes 4194304 | tf_op jit(solution)/shard_map/all_to_all | solution.py:70
  34.3 10.6 %all-to-all-start = ((f32[32,1,128,128]{3,2,1,0:T(8,128)}), f32[32,1,128,128]{3,2,1,0:T(8,128)S(1)}, u32[]{:S(2)}, u32[]{:S(2)}) async-start(f32[32,1,128,128]{3,2,1,0:T(8,128)} %bitcast), calls=%async_computation | async-start | bytes 4194304 | tf_op jit(solution)/shard_map/all_to_all | solution.py:33
  59.0 29.7 %all-to-all-done = f32[32,1,128,128]{3,2,1,0:T(8,128)S(1)} async-done(((f32[32,1,128,128]{3,2,1,0:T(8,128)}), f32[32,1,128,128]{3,2,1,0:T(8,128)S(1)}, u32[]{:S(2)}, u32[]{:S(2)}) %all-to-all-start) | async-done | bytes 2097184 | tf_op jit(solution)/shard_map/all_to_all | solution.py:33
  88.6 14.1 %all-to-all-start.3 = ((f32[256,16,128]{2,1,0:T(8,128)}), f32[256,16,128]{2,1,0:T(8,128)}, u32[]{:S(2)}, u32[]{:S(2)}) async-start(f32[256,16,128]{2,1,0:T(8,128)} %copy.47), calls=%async_computation.3 | async-start | bytes 4194304 | tf_op jit(solution)/shard_map/all_to_all | solution.py:66
  106.1 9.1 %fusion.9 = f32[512,1024]{1,0:T(8,128)S(1)} fusion(f32[1024,512]{0,1:T(8,128)S(1)} %bitcast.108, f32[1024,1024]{1,0:T(8,128)} %param.5), kind=kOutput, calls=%fused_computation.16 | convolution fusion | flops 6442450944 | bytes 8388608 | tf_op jit(solution)/shard_map/ip,mpj->mij/dot_general | solution.py:50
  115.2 3.5 fusion.4
  121.1 7.4 %all-to-all-done.3 = f32[256,16,128]{2,1,0:T(8,128)} async-done(((f32[256,16,128]{2,1,0:T(8,128)}), f32[256,16,128]{2,1,0:T(8,128)}, u32[]{:S(2)}, u32[]{:S(2)}) %all-to-all-start.3) | async-done | bytes 2097184 | tf_op jit(solution)/shard_map/all_to_all | solution.py:66
  128.5 5.0 %all-to-all-start.1 = ((f32[32,1,128,128]{3,2,1,0:T(8,128)}), f32[32,1,128,128]{3,2,1,0:T(8,128)S(1)}, u32[]{:S(2)}, u32[]{:S(2)}) async-start(f32[32,1,128,128]{3,2,1,0:T(8,128)} %bitcast.114), calls=%async_computation.1 | async-start | bytes 4194304 | tf_op jit(solution)/shard_map/all_to_all | solution.py:33
  136.7 48.5 %all-to-all-done.1 = f32[32,1,128,128]{3,2,1,0:T(8,128)S(1)} async-done(((f32[32,1,128,128]{3,2,1,0:T(8,128)}), f32[32,1,128,128]{3,2,1,0:T(8,128)S(1)}, u32[]{:S(2)}, u32[]{:S(2)}) %all-to-all-start.1) | async-done | bytes 2097184 | tf_op jit(solution)/shard_map/all_to_all | solution.py:33
  191.8 4.3 %all-to-all-start.6 = ((f32[32,128,128]{2,0,1:T(8,128)}), f32[32,128,128]{2,0,1:T(8,128)}, u32[]{:S(2)}, u32[]{:S(2)}) async-start(f32[32,128,128]{2,0,1:T(8,128)} %copy.53), calls=%async_computation.6 | async-start | bytes 4194304 | tf_op jit(solution)/shard_map/all_to_all | solution.py:70
  199.3 22.3 %all-to-all-done.6 = f32[32,128,128]{2,0,1:T(8,128)} async-done(((f32[32,128,128]{2,0,1:T(8,128)}), f32[32,128,128]{2,0,1:T(8,128)}, u32[]{:S(2)}, u32[]{:S(2)}) %all-to-all-start.6) | async-done | bytes 2097184 | tf_op jit(solution)/shard_map/all_to_all | solution.py:70
  221.6 5.1 %all-to-all-start.4 = ((f32[32,1,128,128]{3,2,1,0:T(8,128)}), f32[32,1,128,128]{3,2,1,0:T(8,128)S(1)}, u32[]{:S(2)}, u32[]{:S(2)}) async-start(f32[32,1,128,128]{3,2,1,0:T(8,128)} %add.44), calls=%async_computation.4 | async-start | bytes 4194304 | tf_op jit(solution)/shard_map/all_to_all | solution.py:33
  229.5 5.0 %fusion = f32[2048,256]{1,0:T(8,128)} fusion(f32[256,256]{1,0:T(8,128)S(1)} %copy-done.3, f32[32,8,16,128]{3,2,1,0:T(8,128)S(1)} %bitcast.121), kind=kOutput, calls=%fused_computation | convolution fusion | flops 1610612736 | bytes 4456448 | tf_op jit(solution)/shard_map/dot_general | solution.py:65
  237.6 40.7 %all-to-all-done.4 = f32[32,1,128,128]{3,2,1,0:T(8,128)S(1)} async-done(((f32[32,1,128,128]{3,2,1,0:T(8,128)}), f32[32,1,128,128]{3,2,1,0:T(8,128)S(1)}, u32[]{:S(2)}, u32[]{:S(2)}) %all-to-all-start.4) | async-done | bytes 2097184 | tf_op jit(solution)/shard_map/all_to_all | solution.py:33
  278.3 4.3 %all-to-all-start.7 = ((f32[256,16,128]{2,1,0:T(8,128)}), f32[256,16,128]{2,1,0:T(8,128)}, u32[]{:S(2)}, u32[]{:S(2)}) async-start(f32[256,16,128]{2,1,0:T(8,128)} %copy.55), calls=%async_computation.7 | async-start | bytes 4194304 | tf_op jit(solution)/shard_map/all_to_all | solution.py:66
  285.9 9.1 %fusion.10 = f32[512,1024]{1,0:T(8,128)S(1)} fusion(f32[1024,512]{0,1:T(8,128)S(1)} %bitcast.110, f32[1024,1024]{1,0:T(8,128)} %param.5), kind=kOutput, calls=%fused_computation.17 | convolution fusion | flops 6442450944 | bytes 8388608 | tf_op jit(solution)/shard_map/ip,mpj->mij/dot_general | solution.py:50
  295.0 3.5 fusion.3
  300.9 7.2 %all-to-all-done.7 = f32[256,16,128]{2,1,0:T(8,128)} async-done(((f32[256,16,128]{2,1,0:T(8,128)}), f32[256,16,128]{2,1,0:T(8,128)}, u32[]{:S(2)}, u32[]{:S(2)}) %all-to-all-start.7) | async-done | bytes 2097184 | tf_op jit(solution)/shard_map/all_to_all | solution.py:66
  308.1 5.0 %all-to-all-start.5 = ((f32[32,1,128,128]{3,2,1,0:T(8,128)}), f32[32,1,128,128]{3,2,1,0:T(8,128)}, u32[]{:S(2)}, u32[]{:S(2)}) async-start(f32[32,1,128,128]{3,2,1,0:T(8,128)} %bitcast.30), calls=%async_computation.5 | async-start | bytes 4194304 | tf_op jit(solution)/shard_map/all_to_all | solution.py:33
  315.8 52.3 %all-reduce.2 = (f32[]{:T(128)}, f32[]{:T(128)}) all-reduce(f32[]{:T(128)} %multiply_reduce_fusion.1, f32[]{:T(128)} %get-tuple-element.15), channel_id=1, replica_groups=mesh['gx_0'=4,'gx_1'=2,'gy'=4,'gz_0'=2,'gz_1'=4] {'gx_0'}, use_global_device_ids=true, to_apply=%region_1.0 | all-reduce | flops 2 | bytes 16 | tf_op jit(solution)/shard_map/psum | solution.py:40
  371.3 10.9 %all-reduce.1 = (f32[]{:T(128)}, f32[]{:T(128)}) all-reduce(f32[]{:T(128)} %get-tuple-element.13, f32[]{:T(128)} %get-tuple-element.14), channel_id=1, replica_groups=mesh['gx_0'=4,'gx_1'=2,'gy'=4,'gz_0'=2,'gz_1'=4] {'gy'}, use_global_device_ids=true, to_apply=%region_3.0 | all-reduce | flops 2 | bytes 16 | tf_op jit(solution)/shard_map/psum | solution.py:40
  382.2 5.6 %all-reduce.3 = (f32[]{:T(128)}, f32[]{:T(128)}) all-reduce(f32[]{:T(128)} %get-tuple-element.7, f32[]{:T(128)} %get-tuple-element.8), channel_id=1, replica_groups=mesh['gx_0'=4,'gx_1'=2,'gy'=4,'gz_0'=2,'gz_1'=4] {'gz_0'}, use_global_device_ids=true, to_apply=%region_4.0 | all-reduce | flops 2 | bytes 16 | tf_op jit(solution)/shard_map/psum | solution.py:40
  387.9 9.4 %all-reduce = (f32[]{:T(128)}, f32[]{:T(128)}) all-reduce(f32[]{:T(128)} %get-tuple-element.11, f32[]{:T(128)} %get-tuple-element.12), channel_id=1, replica_groups=mesh['gx_0'=4,'gx_1'=2,'gy'=4,'gz_0'=2,'gz_1'=4] {'gz_1'}, use_global_device_ids=true, to_apply=%region_5.0 | all-reduce | flops 2 | bytes 16 | tf_op jit(solution)/shard_map/psum | solution.py:40
  401.9 5.1 %fusion.6 = f32[32,128,128]{2,1,0:T(8,128)} fusion(f32[32,8,16,128]{3,2,1,0:T(8,128)} %copy.56, f32[32,1,128,128]{3,2,1,0:T(8,128)} %all-to-all-done.5, f32[32,128,128]{2,1,0:T(8,128)} %param.4, f32[32,128,128]{2,1,0:T(8,128)S(1)} %copy-done.2, f32[]{:T(128)S(6)} %div.7, f32[]{:T(128)S(6)} %mul_shard_map.3), kind=kLoop, calls=%fused_computation.11 | loop fusion | flops 2621440 | bytes 10485768 | tf_op jit(solution)/shard_map/add | solution.py:80
  (32 shorter events, 56.3 us)
Async XLA Ops:
  0.0 115.2 %copy-start = (f32[512,512]{1,0:T(8,128)S(1)}, f32[512,512]{1,0:T(8,128)}, u32[]{:S(2)}) copy-start(f32[512,512]{1,0:T(8,128)} %param.6) | copy-start | bytes 3145732
  34.3 54.3 %all-to-all-start = ((f32[32,1,128,128]{3,2,1,0:T(8,128)}), f32[32,1,128,128]{3,2,1,0:T(8,128)S(1)}, u32[]{:S(2)}, u32[]{:S(2)}) async-start(f32[32,1,128,128]{3,2,1,0:T(8,128)} %bitcast), calls=%async_computation | async-start | bytes 4194304 | tf_op jit(solution)/shard_map/all_to_all | solution.py:33
  49.9 3.0 copy-start.3
  88.6 39.9 %all-to-all-start.3 = ((f32[256,16,128]{2,1,0:T(8,128)}), f32[256,16,128]{2,1,0:T(8,128)}, u32[]{:S(2)}, u32[]{:S(2)}) async-start(f32[256,16,128]{2,1,0:T(8,128)} %copy.47), calls=%async_computation.3 | async-start | bytes 4194304 | tf_op jit(solution)/shard_map/all_to_all | solution.py:66
  128.5 56.7 %all-to-all-start.1 = ((f32[32,1,128,128]{3,2,1,0:T(8,128)}), f32[32,1,128,128]{3,2,1,0:T(8,128)S(1)}, u32[]{:S(2)}, u32[]{:S(2)}) async-start(f32[32,1,128,128]{3,2,1,0:T(8,128)} %bitcast.114), calls=%async_computation.1 | async-start | bytes 4194304 | tf_op jit(solution)/shard_map/all_to_all | solution.py:33
  187.9 1.3 copy-start.1
  191.8 29.8 %all-to-all-start.6 = ((f32[32,128,128]{2,0,1:T(8,128)}), f32[32,128,128]{2,0,1:T(8,128)}, u32[]{:S(2)}, u32[]{:S(2)}) async-start(f32[32,128,128]{2,0,1:T(8,128)} %copy.53), calls=%async_computation.6 | async-start | bytes 4194304 | tf_op jit(solution)/shard_map/all_to_all | solution.py:70
  221.6 56.7 %all-to-all-start.4 = ((f32[32,1,128,128]{3,2,1,0:T(8,128)}), f32[32,1,128,128]{3,2,1,0:T(8,128)S(1)}, u32[]{:S(2)}, u32[]{:S(2)}) async-start(f32[32,1,128,128]{3,2,1,0:T(8,128)} %add.44), calls=%async_computation.4 | async-start | bytes 4194304 | tf_op jit(solution)/shard_map/all_to_all | solution.py:33
  278.3 29.8 %all-to-all-start.7 = ((f32[256,16,128]{2,1,0:T(8,128)}), f32[256,16,128]{2,1,0:T(8,128)}, u32[]{:S(2)}, u32[]{:S(2)}) async-start(f32[256,16,128]{2,1,0:T(8,128)} %copy.55), calls=%async_computation.7 | async-start | bytes 4194304 | tf_op jit(solution)/shard_map/all_to_all | solution.py:66
  308.1 93.8 %all-to-all-start.5 = ((f32[32,1,128,128]{3,2,1,0:T(8,128)}), f32[32,1,128,128]{3,2,1,0:T(8,128)}, u32[]{:S(2)}, u32[]{:S(2)}) async-start(f32[32,1,128,128]{3,2,1,0:T(8,128)} %bitcast.30), calls=%async_computation.5 | async-start | bytes 4194304 | tf_op jit(solution)/shard_map/all_to_all | solution.py:33
  398.5 3.4 copy-start.2
where the time goes:
time: 408 us; the launch traced here: 407 us
  waiting for transfers between devices  156 us (38%)
  blocking collectives  113 us (28%)
  starting transfers between devices  48.4 us (12%)
  local copies, waits for them, and re-layouts  41 us (10%)
  matrix products  33.8 us (8%)
  other arithmetic  13.7 us (3%)
    all_to_all x4, waiting for transfers between devices, joined_exchange(): tiles = lax.all_to_all(tiles, axis, split_axis=0, concat_axis=0, tiled=True)  119 us
    psum x5, blocking collectives, over_axes(): value = lax.psum(value, axis)  81.4 us
    all_to_all x1, blocking collectives, apply_block(): lax.all_to_all(tensor, GZ, split_axis=1, concat_axis=0, tiled=True)  31.4 us
    all_to_all x4, starting transfers between devices, joined_exchange(): tiles = lax.all_to_all(tiles, axis, split_axis=0, concat_axis=0, tiled=True)  25.7 us
    all_to_all x1, waiting for transfers between devices, apply_block(): lax.all_to_all(tensor, GZ, split_axis=1, concat_axis=0, tiled=True)  22.3 us
    all_to_all x2, starting transfers between devices, fibre_product(): return lax.all_to_all(product, GZ, split_axis=0, concat_axis=1, tiled=True)  18.4 us
    dot_general x2, matrix products, slab_products(): along_one = jnp.einsum('ip,mpj->mij', factor_a, slabs, precision=highest)  18.1 us
    all_to_all x2, waiting for transfers between devices, fibre_product(): return lax.all_to_all(product, GZ, split_axis=0, concat_axis=1, tiled=True)  14.6 us
  transfers between devices with their start and end apart: 7, of which 6 were waited for; matrix products, arithmetic and copies ran while one was open for 18% of the time, Pallas kernels for 0%

commit v1 on v0

--- a/solution.py
+++ b/solution.py
@@ -37,7 +37,8 @@
 
 def over_axes(value, axes):
     for axis in axes:
-        value = lax.psum(value, axis)
+        parts = lax.all_gather(value, axis)
+        value = jnp.sum(parts, axis=0)
     return value
 
 

time: 408 us -> 430 us (1.054); the launches traced: 407 us -> 423 us
  local copies, waits for them, and re-layouts: 41 us -> 57.1 us
  blocking collectives: 113 us -> 106 us
  other arithmetic: 13.7 us -> 20.1 us
    psum x5 -> x0, blocking collectives: 81.4 us -> none  [over_axes(): value = lax.psum(value, axis)]
    unnamed x0 -> x5, blocking collectives: none -> 74.2 us
    unnamed x12 -> x47, local copies, waits for them, and re-layouts: 7.37 us -> 23.5 us
    reduce_sum x0 -> x10, other arithmetic: none -> 6.39 us  [over_axes(): value = jnp.sum(parts, axis=0)]
  transfers between devices with their start and end apart: 7 -> 7, of which waited for: 6 -> 6; matrix products, arithmetic and copies ran while one was open for 18% -> 23% of each run, Pallas kernels for 0% -> 0%
where the time goes in v1:
time: 430 us; the launch traced here: 423 us
  waiting for transfers between devices  156 us (36%)
  blocking collectives  106 us (25%)
  local copies, waits for them, and re-layouts  57.1 us (13%)
  starting transfers between devices  48.7 us (11%)
  matrix products  33.8 us (8%)
  other arithmetic  20.1 us (5%)
    all_to_all x4, waiting for transfers between devices, joined_exchange(): tiles = lax.all_to_all(tiles, axis, split_axis=0, concat_axis=0, tiled=True)  119 us
    unnamed x5, blocking collectives  74.2 us
    all_to_all x1, blocking collectives, apply_block(): lax.all_to_all(tensor, GZ, split_axis=1, concat_axis=0, tiled=True)  31.4 us
    all_to_all x4, starting transfers between devices, joined_exchange(): tiles = lax.all_to_all(tiles, axis, split_axis=0, concat_axis=0, tiled=True)  25.8 us
    unnamed x47, local copies, waits for them, and re-layouts  23.5 us
    all_to_all x1, waiting for transfers between devices, apply_block(): lax.all_to_all(tensor, GZ, split_axis=1, concat_axis=0, tiled=True)  22.2 us
    all_to_all x2, starting transfers between devices, fibre_product(): return lax.all_to_all(product, GZ, split_axis=0, concat_axis=1, tiled=True)  18.7 us
    dot_general x2, matrix products, slab_products(): along_one = jnp.einsum('ip,mpj->mij', factor_a, slabs, precision=highest)  18.1 us
  transfers between devices with their start and end apart: 7, of which 6 were waited for; matrix products, arithmetic and copies ran while one was open for 23% of the time, Pallas kernels for 0%

profile of v1, /device:TPU:32, one launch (start us, length us, event | category | flops | bytes accessed | tf_op | source)
XLA Modules:
  0.0 423.0 jit_solution(13523386483845049515)
XLA Ops:
  2.9 31.4 %all_to_all.89 = f32[32,128,128]{2,0,1:T(8,128)} all-to-all(f32[32,128,128]{2,0,1:T(8,128)S(1)} %copy.44), channel_id=1, replica_groups=mesh['gx_0'=4,'gx_1'=2,'gy'=4,'gz_0'=2,'gz_1'=4] {'gz_0','gz_1'}, dimensions={1} | all-to-all | bytes 4194304 | tf_op jit(solution)/shard_map/all_to_all | solution.py:71
  34.3 10.6 %all-to-all-start = ((f32[32,1,128,128]{3,2,1,0:T(8,128)}), f32[32,1,128,128]{3,2,1,0:T(8,128)S(1)}, u32[]{:S(2)}, u32[]{:S(2)}) async-start(f32[32,1,128,128]{3,2,1,0:T(8,128)} %bitcast.10), calls=%async_computation | async-start | bytes 4194304 | tf_op jit(solution)/shard_map/all_to_all | solution.py:33
  59.0 29.6 %all-to-all-done = f32[32,1,128,128]{3,2,1,0:T(8,128)S(1)} async-done(((f32[32,1,128,128]{3,2,1,0:T(8,128)}), f32[32,1,128,128]{3,2,1,0:T(8,128)S(1)}, u32[]{:S(2)}, u32[]{:S(2)}) %all-to-all-start) | async-done | bytes 2097184 | tf_op jit(solution)/shard_map/all_to_all | solution.py:33
  88.6 14.4 %all-to-all-start.3 = ((f32[256,16,128]{2,1,0:T(8,128)}), f32[256,16,128]{2,1,0:T(8,128)}, u32[]{:S(2)}, u32[]{:S(2)}) async-start(f32[256,16,128]{2,1,0:T(8,128)} %copy.47), calls=%async_computation.3 | async-start | bytes 4194304 | tf_op jit(solution)/shard_map/all_to_all | solution.py:67
  106.4 9.1 %fusion.9 = f32[512,1024]{1,0:T(8,128)S(1)} fusion(f32[1024,512]{0,1:T(8,128)S(1)} %bitcast.123, f32[1024,1024]{1,0:T(8,128)} %param.5), kind=kOutput, calls=%fused_computation.16 | convolution fusion | flops 6442450944 | bytes 8388608 | tf_op jit(solution)/shard_map/ip,mpj->mij/dot_general | solution.py:51
  115.4 3.5 fusion.4
  121.3 7.4 %all-to-all-done.3 = f32[256,16,128]{2,1,0:T(8,128)} async-done(((f32[256,16,128]{2,1,0:T(8,128)}), f32[256,16,128]{2,1,0:T(8,128)}, u32[]{:S(2)}, u32[]{:S(2)}) %all-to-all-start.3) | async-done | bytes 2097184 | tf_op jit(solution)/shard_map/all_to_all | solution.py:67
  128.7 5.0 %all-to-all-start.1 = ((f32[32,1,128,128]{3,2,1,0:T(8,128)}), f32[32,1,128,128]{3,2,1,0:T(8,128)S(1)}, u32[]{:S(2)}, u32[]{:S(2)}) async-start(f32[32,1,128,128]{3,2,1,0:T(8,128)} %bitcast.129), calls=%async_computation.1 | async-start | bytes 4194304 | tf_op jit(solution)/shard_map/all_to_all | solution.py:33
  136.9 48.5 %all-to-all-done.1 = f32[32,1,128,128]{3,2,1,0:T(8,128)S(1)} async-done(((f32[32,1,128,128]{3,2,1,0:T(8,128)}), f32[32,1,128,128]{3,2,1,0:T(8,128)S(1)}, u32[]{:S(2)}, u32[]{:S(2)}) %all-to-all-start.1) | async-done | bytes 2097184 | tf_op jit(solution)/shard_map/all_to_all | solution.py:33
  192.0 4.3 %all-to-all-start.6 = ((f32[32,128,128]{2,0,1:T(8,128)}), f32[32,128,128]{2,0,1:T(8,128)}, u32[]{:S(2)}, u32[]{:S(2)}) async-start(f32[32,128,128]{2,0,1:T(8,128)} %copy.53), calls=%async_computation.6 | async-start | bytes 4194304 | tf_op jit(solution)/shard_map/all_to_all | solution.py:71
  199.5 22.2 %all-to-all-done.6 = f32[32,128,128]{2,0,1:T(8,128)} async-done(((f32[32,128,128]{2,0,1:T(8,128)}), f32[32,128,128]{2,0,1:T(8,128)}, u32[]{:S(2)}, u32[]{:S(2)}) %all-to-all-start.6) | async-done | bytes 2097184 | tf_op jit(solution)/shard_map/all_to_all | solution.py:71
  221.7 5.1 %all-to-all-start.4 = ((f32[32,1,128,128]{3,2,1,0:T(8,128)}), f32[32,1,128,128]{3,2,1,0:T(8,128)S(1)}, u32[]{:S(2)}, u32[]{:S(2)}) async-start(f32[32,1,128,128]{3,2,1,0:T(8,128)} %add.24), calls=%async_computation.4 | async-start | bytes 4194304 | tf_op jit(solution)/shard_map/all_to_all | solution.py:33
  229.7 5.0 %fusion = f32[2048,256]{1,0:T(8,128)} fusion(f32[256,256]{1,0:T(8,128)S(1)} %copy-done.3, f32[32,8,16,128]{3,2,1,0:T(8,128)S(1)} %bitcast.136), kind=kOutput, calls=%fused_computation | convolution fusion | flops 1610612736 | bytes 4456448 | tf_op jit(solution)/shard_map/dot_general | solution.py:66
  237.7 40.9 %all-to-all-done.4 = f32[32,1,128,128]{3,2,1,0:T(8,128)S(1)} async-done(((f32[32,1,128,128]{3,2,1,0:T(8,128)}), f32[32,1,128,128]{3,2,1,0:T(8,128)S(1)}, u32[]{:S(2)}, u32[]{:S(2)}) %all-to-all-start.4) | async-done | bytes 2097184 | tf_op jit(solution)/shard_map/all_to_all | solution.py:33
  278.6 4.3 %all-to-all-start.7 = ((f32[256,16,128]{2,1,0:T(8,128)}), f32[256,16,128]{2,1,0:T(8,128)}, u32[]{:S(2)}, u32[]{:S(2)}) async-start(f32[256,16,128]{2,1,0:T(8,128)} %copy.55), calls=%async_computation.7 | async-start | bytes 4194304 | tf_op jit(solution)/shard_map/all_to_all | solution.py:67
  286.3 9.1 %fusion.10 = f32[512,1024]{1,0:T(8,128)S(1)} fusion(f32[1024,512]{0,1:T(8,128)S(1)} %bitcast.125, f32[1024,1024]{1,0:T(8,128)} %param.5), kind=kOutput, calls=%fused_computation.17 | convolution fusion | flops 6442450944 | bytes 8388608 | tf_op jit(solution)/shard_map/ip,mpj->mij/dot_general | solution.py:51
  295.4 3.5 fusion.3
  301.3 7.2 %all-to-all-done.7 = f32[256,16,128]{2,1,0:T(8,128)} async-done(((f32[256,16,128]{2,1,0:T(8,128)}), f32[256,16,128]{2,1,0:T(8,128)}, u32[]{:S(2)}, u32[]{:S(2)}) %all-to-all-start.7) | async-done | bytes 2097184 | tf_op jit(solution)/shard_map/all_to_all | solution.py:67
  308.4 5.1 %all-to-all-start.5 = ((f32[32,1,128,128]{3,2,1,0:T(8,128)}), f32[32,1,128,128]{3,2,1,0:T(8,128)}, u32[]{:S(2)}, u32[]{:S(2)}) async-start(f32[32,1,128,128]{3,2,1,0:T(8,128)} %bitcast.45), calls=%async_computation.5 | async-start | bytes 4194304 | tf_op jit(solution)/shard_map/all_to_all | solution.py:33
  320.1 47.9 %all-reduce.12 = (f32[4]{0:T(128)S(1)}, f32[4]{0:T(128)S(1)}) all-reduce(f32[4]{0:T(128)S(1)} %dynamic-update-slice, f32[4]{0:T(128)S(1)} %dynamic-update-slice.5), channel_id=1, replica_groups=mesh['gx_0'=4,'gx_1'=2,'gy'=4,'gz_0'=2,'gz_1'=4] {'gx_0'}, use_global_device_ids=true, to_apply=%add | all-reduce | flops 8 | bytes 64
  379.5 10.2 %all-reduce.11 = (f32[4]{0:T(128)S(1)}, f32[4]{0:T(128)S(1)}) all-reduce(f32[4]{0:T(128)S(1)} %dynamic-update-slice.2, f32[4]{0:T(128)S(1)} %dynamic-update-slice.7), channel_id=1, replica_groups=mesh['gx_0'=4,'gx_1'=2,'gy'=4,'gz_0'=2,'gz_1'=4] {'gy'}, use_global_device_ids=true, to_apply=%add.2 | all-reduce | flops 8 | bytes 64
  394.3 4.9 %all-reduce.13 = (f32[2]{0:T(128)S(1)}, f32[2]{0:T(128)S(1)}) all-reduce(f32[2]{0:T(128)S(1)} %dynamic-update-slice.3, f32[2]{0:T(128)S(1)} %dynamic-update-slice.8), channel_id=1, replica_groups=mesh['gx_0'=4,'gx_1'=2,'gy'=4,'gz_0'=2,'gz_1'=4] {'gz_0'}, use_global_device_ids=true, to_apply=%add.3 | all-reduce | flops 4 | bytes 32
  403.1 8.7 %all-reduce.10 = (f32[4]{0:T(128)S(1)}, f32[4]{0:T(128)S(1)}) all-reduce(f32[4]{0:T(128)S(1)} %dynamic-update-slice.4, f32[4]{0:T(128)S(1)} %dynamic-update-slice.9), channel_id=1, replica_groups=mesh['gx_0'=4,'gx_1'=2,'gy'=4,'gz_0'=2,'gz_1'=4] {'gz_1'}, use_global_device_ids=true, to_apply=%add.4 | all-reduce | flops 8 | bytes 64
  417.6 5.1 %fusion.6 = f32[32,128,128]{2,1,0:T(8,128)} fusion(f32[32,8,16,128]{3,2,1,0:T(8,128)} %copy.56, f32[32,1,128,128]{3,2,1,0:T(8,128)} %all-to-all-done.5, f32[32,128,128]{2,1,0:T(8,128)} %param.4, f32[32,128,128]{2,1,0:T(8,128)S(1)} %copy-done.2, f32[]{:T(128)S(6)} %div.7, f32[]{:T(128)S(6)} %mul_shard_map.3), kind=kLoop, calls=%fused_computation.11 | loop fusion | flops 2621440 | bytes 10485768 | tf_op jit(solution)/shard_map/add | solution.py:81
  (77 shorter events, 78.1 us)
Async XLA Ops:
  0.0 115.4 %copy-start = (f32[512,512]{1,0:T(8,128)S(1)}, f32[512,512]{1,0:T(8,128)}, u32[]{:S(2)}) copy-start(f32[512,512]{1,0:T(8,128)} %param.6) | copy-start | bytes 3145732
  34.3 54.3 %all-to-all-start = ((f32[32,1,128,128]{3,2,1,0:T(8,128)}), f32[32,1,128,128]{3,2,1,0:T(8,128)S(1)}, u32[]{:S(2)}, u32[]{:S(2)}) async-start(f32[32,1,128,128]{3,2,1,0:T(8,128)} %bitcast.10), calls=%async_computation | async-start | bytes 4194304 | tf_op jit(solution)/shard_map/all_to_all | solution.py:33
  49.9 3.0 copy-start.3
  88.6 40.1 %all-to-all-start.3 = ((f32[256,16,128]{2,1,0:T(8,128)}), f32[256,16,128]{2,1,0:T(8,128)}, u32[]{:S(2)}, u32[]{:S(2)}) async-start(f32[256,16,128]{2,1,0:T(8,128)} %copy.47), calls=%async_computation.3 | async-start | bytes 4194304 | tf_op jit(solution)/shard_map/all_to_all | solution.py:67
  128.7 56.7 %all-to-all-start.1 = ((f32[32,1,128,128]{3,2,1,0:T(8,128)}), f32[32,1,128,128]{3,2,1,0:T(8,128)S(1)}, u32[]{:S(2)}, u32[]{:S(2)}) async-start(f32[32,1,128,128]{3,2,1,0:T(8,128)} %bitcast.129), calls=%async_computation.1 | async-start | bytes 4194304 | tf_op jit(solution)/shard_map/all_to_all | solution.py:33
  188.1 1.4 copy-start.1
  192.0 29.7 %all-to-all-start.6 = ((f32[32,128,128]{2,0,1:T(8,128)}), f32[32,128,128]{2,0,1:T(8,128)}, u32[]{:S(2)}, u32[]{:S(2)}) async-start(f32[32,128,128]{2,0,1:T(8,128)} %copy.53), calls=%async_computation.6 | async-start | bytes 4194304 | tf_op jit(solution)/shard_map/all_to_all | solution.py:71
  221.7 56.9 %all-to-all-start.4 = ((f32[32,1,128,128]{3,2,1,0:T(8,128)}), f32[32,1,128,128]{3,2,1,0:T(8,128)S(1)}, u32[]{:S(2)}, u32[]{:S(2)}) async-start(f32[32,1,128,128]{3,2,1,0:T(8,128)} %add.24), calls=%async_computation.4 | async-start | bytes 4194304 | tf_op jit(solution)/shard_map/all_to_all | solution.py:33
  278.6 29.8 %all-to-all-start.7 = ((f32[256,16,128]{2,1,0:T(8,128)}), f32[256,16,128]{2,1,0:T(8,128)}, u32[]{:S(2)}, u32[]{:S(2)}) async-start(f32[256,16,128]{2,1,0:T(8,128)} %copy.55), calls=%async_computation.7 | async-start | bytes 4194304 | tf_op jit(solution)/shard_map/all_to_all | solution.py:67
  308.4 5.1 %copy-start.8 = (u32[256]{0:T(256)S(1)}, u32[256]{0:T(256)}, u32[]{:S(2)}) copy-start(u32[256]{0:T(256)} %constant.13) | copy-start | bytes 3076
  308.4 109.2 %all-to-all-start.5 = ((f32[32,1,128,128]{3,2,1,0:T(8,128)}), f32[32,1,128,128]{3,2,1,0:T(8,128)}, u32[]{:S(2)}, u32[]{:S(2)}) async-start(f32[32,1,128,128]{3,2,1,0:T(8,128)} %bitcast.45), calls=%async_computation.5 | async-start | bytes 4194304 | tf_op jit(solution)/shard_map/all_to_all | solution.py:33
  313.5 6.0 %copy-start.7 = (u32[256]{0:T(256)S(1)}, u32[256]{0:T(256)}, u32[]{:S(2)}) copy-start(u32[256]{0:T(256)} %constant.18) | copy-start | bytes 3076
  313.5 58.4 %copy-start.6 = (u32[256]{0:T(256)S(1)}, u32[256]{0:T(256)}, u32[]{:S(2)}) copy-start(u32[256]{0:T(256)} %constant.23) | copy-start | bytes 3076
  313.5 65.4 %copy-start.5 = (u32[256]{0:T(256)S(1)}, u32[256]{0:T(256)}, u32[]{:S(2)}) copy-start(u32[256]{0:T(256)} %constant.28) | copy-start | bytes 3076
  313.6 80.1 %copy-start.4 = (u32[256]{0:T(256)S(1)}, u32[256]{0:T(256)}, u32[]{:S(2)}) copy-start(u32[256]{0:T(256)} %constant.33) | copy-start | bytes 3076
  414.2 3.4 copy-start.2
